TPU v7x, 32 devices: a whole 2x2x4 slice. The times are simulated.
32 devices in a mesh: dp: 4 (over y, x), expert: 4 (over z), tensor: 2 (over core).
Axes of the slice: x: 2, y: 2, z: 4, core: 2. Of those that a mesh axis runs over, the one named last changes fastest.
Arguments:
- tokens: bfloat16 [1, 256, 3584], P(None, ('dp', 'expert'), 'tensor'), may hold values from -6 to 6
- gate_weight: bfloat16 [16, 3584, 1024], P(('dp', 'expert'), None, 'tensor'), may hold values from -0.09375 to 0.09375
- up_weight: bfloat16 [16, 3584, 1024], P(('dp', 'expert'), None, 'tensor'), may hold values from -0.09375 to 0.09375
- down_weight: bfloat16 [16, 1024, 3584], P(('dp', 'expert'), 'tensor'), may hold values from -0.1875 to 0.1875
- expert_ids: int32 [1, 256, 8], P(None, ('dp', 'expert')), may hold values from 0 to 15, all different within a row; in each aligned block of 16 rows (0 to 15, 16 to 31, ..., all dimensions but the last counted through in order) at most 16 rows name the same one
- gate_codes: int32 [1, 256, 8], P(None, ('dp', 'expert')), may hold values from 1 to 32767
Outputs:
- mixed: bfloat16 [1, 256, 3584], P(None, ('dp', 'expert'), 'tensor')
Inputs may be any that keep to these rules, and one draw needn't show every extreme that they name: `expert_ids`: the 8 experts of one token differ. For every step, of the 16 tokens that one index of dp+expert holds, no expert is named by more than 16.
All inputs are finite; a program needn't handle non-finite values.
Results may differ from a plain program's by a relative error of at most 0.0095.
Values may be sent and summed in bfloat16 or wider, within the bound.
A program may use at most 64 MiB of HBM per device.

v0:
```python
import jax
import jax.numpy as jnp
from jax import lax
from jax.sharding import PartitionSpec as P


def local(tokens, gate_weight, up_weight, down_weight, expert_ids, gate_codes):
    owners = lax.axis_size("dp") * lax.axis_size("expert")
    tok_rows = tokens.shape[1]
    top_count = expert_ids.shape[2]
    slot_depth = min(tok_rows, max(2, 2 * tok_rows * top_count // owners))
    slot_count = owners * slot_depth
    w_gate = gate_weight[0]
    w_up = up_weight[0]
    w_down = down_weight[0]
    slot_numbers = jnp.arange(slot_count, dtype=jnp.int32)
    owner_numbers = jnp.arange(owners, dtype=jnp.int32)
    step_tokens = tokens[0]
    route_ids = expert_ids[0].reshape(tok_rows * top_count)
    onehot = (route_ids[:, None] == owner_numbers[None, :]).astype(jnp.int32)
    before = jnp.cumsum(onehot, axis=0) - onehot
    slot_rank = jnp.sum(before * onehot, axis=1)
    slot_index = route_ids * slot_depth + slot_rank
    select = (slot_index[:, None] == slot_numbers[None, :]).astype(jnp.bfloat16)
    per_token = jnp.sum(select.reshape(tok_rows, top_count, slot_count), axis=1)
    packed = jnp.einsum(
        "ts,td->sd", per_token, step_tokens, preferred_element_type=jnp.float32
    ).astype(jnp.bfloat16)
    packed = packed.reshape(owners, slot_depth, step_tokens.shape[1])
    arrived = lax.all_to_all(packed, ("dp", "expert"), split_axis=0, concat_axis=0, tiled=True)
    owner_rows = arrived.reshape(slot_count, step_tokens.shape[1])
    owner_rows = lax.all_gather(owner_rows, "tensor", axis=1, tiled=True)
    gated = jnp.dot(owner_rows, w_gate, preferred_element_type=jnp.float32)
    lifted = jnp.dot(owner_rows, w_up, preferred_element_type=jnp.float32)
    hidden = (jax.nn.silu(gated) * lifted).astype(jnp.bfloat16)
    partial_value = jnp.dot(hidden, w_down, preferred_element_type=jnp.float32).astype(jnp.bfloat16)
    summed = (
        lax.psum_scatter(partial_value, "tensor", scatter_dimension=1, tiled=True)
        .astype(jnp.float32)
        .astype(jnp.bfloat16)
    )
    half_width = summed.shape[1]
    result = summed.reshape(owners, slot_depth, half_width)
    returned = lax.all_to_all(result, ("dp", "expert"), split_axis=0, concat_axis=0, tiled=True)
    returned = returned.reshape(slot_count, half_width)
    picked = jnp.dot(select, returned, preferred_element_type=jnp.float32)
    codes = gate_codes[0].astype(jnp.float32)
    shares = codes / jnp.sum(codes, axis=1, keepdims=True)
    mixed_rows = jnp.sum(
        picked.reshape(tok_rows, top_count, half_width) * shares[:, :, None], axis=1
    )
    outputs = [mixed_rows.astype(jnp.bfloat16)]
    return jnp.stack(outputs)


def solution(mesh):
    in_specs = (
        P(None, ("dp", "expert"), "tensor"),
        P(("dp", "expert"), None, "tensor"),
        P(("dp", "expert"), None, "tensor"),
        P(("dp", "expert"), "tensor", None),
        P(None, ("dp", "expert"), None),
        P(None, ("dp", "expert"), None),
    )
    out_specs = P(None, ("dp", "expert"), "tensor")
    return jax.shard_map(local, mesh=mesh, in_specs=in_specs, out_specs=out_specs, check_vma=False)
```

profile of v0, /device:TPU:0, one launch (start us, length us, event | category | flops | bytes accessed | tf_op | source)
XLA Modules:
  0.0 110.7 jit_solution(10478560798243014809)
XLA Ops:
  6.5 0.0 copy-start
  6.5 0.0 all-gather.2.cloned.1.call-start
  6.5 0.8 copy.17
  7.3 0.1 eq.51
  7.4 0.1 fusion.25
  7.5 0.2 reduce_window_sum.11
  7.7 0.2 select_reduce_fusion
  7.8 0.1 reduce_sum.42
  7.9 0.1 copy.18
  8.0 0.7 bitcast_add_fusion
  8.7 0.1 copy.19
  8.8 0.1 fusion.23
  8.9 0.0 copy-done
  8.9 0.4 convolution_convert_fusion.1
  9.3 32.9 %all_to_all.10 = bf16[16,16,1792]{2,1,0:T(8,128)(2,1)} all-to-all(bf16[16,16,1792]{2,1,0:T(8,128)(2,1)S(1)} %bitcast.39), channel_id=1, replica_groups=mesh['dp'=4,'expert'=4,'tensor'=2] {'dp','expert'}, dimensions={0} | all-to-all | bytes 1835008 | tf_op jit(solution)/shard_map/all_to_all | solution.py:30
  42.2 0.0 all-gather.2.cloned.1.call-update
  42.2 0.0 reduce-scatter.2.cloned.1.call-start
  42.3 7.5 %all-gather.2.cloned.1.call-done = bf16[256,3584]{1,0:T(8,128)(2,1)} async-done(((bf16[256,1792]{1,0:T(8,128)(2,1)}), bf16[256,3584]{1,0:T(8,128)(2,1)}) %all-gather.2.cloned.1.call-update) | async-done | bytes 1835024 | tf_op jit(solution)/shard_map/all_gather | solution.py:32
  49.8 0.0 copy-start.2
  49.8 3.8 %fusion.3 = f32[256,512]{1,0:T(8,128)S(1)} fusion(bf16[256,3584]{1,0:T(8,128)(2,1)} %all-gather.2.cloned.1.call-done, bf16[1,3584,512]{2,1,0:T(8,128)(2,1)} %param.7), kind=kOutput, calls=%fused_computation.4 | convolution fusion | flops 939524096 | bytes 6029312 | tf_op jit(solution)/shard_map/dot_general | solution.py:33
  53.6 0.0 copy-done.2
  53.7 6.6 %convolution_convert_fusion = bf16[256,3584]{1,0:T(8,128)(2,1)} fusion(bf16[1,512,3584]{2,1,0:T(8,128)(2,1)} %param.9, bf16[256,3584]{1,0:T(8,128)(2,1)S(1)} %copy-done.2, bf16[1,3584,512]{2,1,0:T(8,128)(2,1)} %param.8, f32[256,512]{1,0:T(8,128)S(1)} %fusion.3), kind=kOutput, calls=%fused_computation | convolution fusion | flops 1880752128 | bytes 11534336 | tf_op jit(solution)/shard_map/dot_general | solution.py:36
  60.2 0.0 copy-start.1
  60.2 0.0 reduce-scatter.2.cloned.1.call-update
  60.2 10.6 %reduce-scatter.2.cloned.1.call-done = bf16[256,1792]{1,0:T(8,128)(2,1)} async-done(((bf16[256,3584]{1,0:T(8,128)(2,1)}), bf16[256,1792]{1,0:T(8,128)(2,1)}) %reduce-scatter.2.cloned.1.call-update) | async-done | bytes 917520 | tf_op jit(solution)/shard_map/reduce_scatter | solution.py:38
  70.9 6.9 %all-to-all-start.1 = ((bf16[16,16,1792]{2,1,0:T(8,128)(2,1)}), bf16[16,16,1792]{2,1,0:T(8,128)(2,1)S(1)}, u32[]{:S(2)}, u32[]{:S(2)}) async-start(bf16[16,16,1792]{2,1,0:T(8,128)(2,1)} %bitcast.40), calls=%async_computation.2 | async-start | bytes 1835008 | tf_op jit(solution)/shard_map/all_to_all | solution.py:44
  77.8 0.0 copy-done.1
  77.8 0.1 copy.21
  77.9 24.9 %all-to-all-done.1 = bf16[16,16,1792]{2,1,0:T(8,128)(2,1)S(1)} async-done(((bf16[16,16,1792]{2,1,0:T(8,128)(2,1)}), bf16[16,16,1792]{2,1,0:T(8,128)(2,1)S(1)}, u32[]{:S(2)}, u32[]{:S(2)}) %all-to-all-start.1) | async-done | bytes 917536 | tf_op jit(solution)/shard_map/all_to_all | solution.py:44
  102.8 1.1 fusion.8
  (2 shorter events, 0.0 us)
Async XLA Ops:
  6.5 2.4 %copy-start = (bf16[1,16,1792]{2,1,0:T(8,128)(2,1)S(1)}, bf16[1,16,1792]{2,1,0:T(8,128)(2,1)}, u32[]{:S(2)}) copy-start(bf16[1,16,1792]{2,1,0:T(8,128)(2,1)} %param.6) | copy-start | bytes 172036
  6.5 43.3 %all-gather.2.cloned.1.call-start = ((), (), s32[]{:S(2)}) async-start(), calls=%async_computation.3 | async-start | bytes 2752512 | tf_op jit(solution)/shard_map/all_gather | solution.py:32
  42.2 28.6 %reduce-scatter.2.cloned.1.call-start = ((), (), s32[]{:S(2)}) async-start(), calls=%async_computation.4 | async-start | bytes 2752512 | tf_op jit(solution)/shard_map/reduce_scatter | solution.py:38
  49.8 3.8 %copy-start.2 = (bf16[256,3584]{1,0:T(8,128)(2,1)S(1)}, bf16[256,3584]{1,0:T(8,128)(2,1)}, u32[]{:S(2)}) copy-start(bf16[256,3584]{1,0:T(8,128)(2,1)} %all-gather.2.cloned.1.call-done) | copy-start | bytes 5505028
  60.2 17.6 %copy-start.1 = (s32[1,16,8]{1,2,0:T(8,128)S(1)}, s32[1,16,8]{1,2,0:T(8,128)}, u32[]{:S(2)}) copy-start(s32[1,16,8]{1,2,0:T(8,128)} %param.11) | copy-start | bytes 1540
  70.9 31.9 %all-to-all-start.1 = ((bf16[16,16,1792]{2,1,0:T(8,128)(2,1)}), bf16[16,16,1792]{2,1,0:T(8,128)(2,1)S(1)}, u32[]{:S(2)}, u32[]{:S(2)}) async-start(bf16[16,16,1792]{2,1,0:T(8,128)(2,1)} %bitcast.40), calls=%async_computation.2 | async-start | bytes 1835008 | tf_op jit(solution)/shard_map/all_to_all | solution.py:44
Sparse Core Ops, SparseCore 0:
  42.4 7.3 all-gather.1
  60.4 10.4 reduce-scatter.1
where the time goes:
time: 111 us
  waiting for transfers between devices  43 us (39%)
  blocking collectives  32.9 us (30%)
  between operations  13.5 us (12%)
  matrix products  11.9 us (11%)
  starting transfers between devices  6.97 us (6%)
  other arithmetic  1.28 us (1%)
  local copies, waits for them, and re-layouts  1.18 us (1%)
    all_to_all x1, blocking collectives, local(): lax.all_to_all(packed, ('dp', 'expert'), split_axis=0, concat_axis=0, til...  32.9 us
    all_to_all x1, waiting for transfers between devices, local(): lax.all_to_all(result, ('dp', 'expert'), split_axis=0, concat_axis=0, til...  24.9 us
    reduce_scatter x1, waiting for transfers between devices, local(): lax.psum_scatter(partial_value, 'tensor', scatter_dimension=1, tiled=True)  10.6 us
    all_gather x1, waiting for transfers between devices, local(): owner_rows = lax.all_gather(owner_rows, 'tensor', axis=1, tiled=True)  7.52 us
    all_to_all x1, starting transfers between devices, local(): lax.all_to_all(result, ('dp', 'expert'), split_axis=0, concat_axis=0, til...  6.92 us
    dot_general x1, matrix products, local(): jnp.dot(hidden, w_down, preferred_element_type=jnp.float32)  6.57 us
    dot_general x1, matrix products, local(): gated = jnp.dot(owner_rows, w_gate, preferred_element_type=jnp.float32)  3.82 us
  transfers between devices with their start and end apart: 3, of which 3 were waited for; matrix products, arithmetic and copies ran while one was open for 0% of the time, Pallas kernels for 0%

commit v1 on v0

--- a/solution.py
+++ b/solution.py
@@ -29,7 +29,7 @@
     packed = packed.reshape(owners, slot_depth, step_tokens.shape[1])
     arrived = lax.all_to_all(packed, ("dp", "expert"), split_axis=0, concat_axis=0, tiled=True)
     owner_rows = arrived.reshape(slot_count, step_tokens.shape[1])
-    owner_rows = lax.all_gather(owner_rows, "tensor", axis=1, tiled=True)
+    owner_rows = jnp.concatenate(lax.all_gather(owner_rows, "tensor"), axis=1)
     gated = jnp.dot(owner_rows, w_gate, preferred_element_type=jnp.float32)
     lifted = jnp.dot(owner_rows, w_up, preferred_element_type=jnp.float32)
     hidden = (jax.nn.silu(gated) * lifted).astype(jnp.bfloat16)

time: 111 us -> 113 us (1.018)
  local copies, waits for them, and re-layouts: 1.18 us -> 3.97 us
    all_gather x0 -> x1, local copies, waits for them, and re-layouts: none -> 2.8 us  [local(): owner_rows = jnp.concatenate(lax.all_gather(owner_rows, 'tensor'), axis=1)]
where the time goes in v1:
time: 113 us
  waiting for transfers between devices  43 us (38%)
  blocking collectives  32.9 us (29%)
  between operations  13.5 us (12%)
  matrix products  11.3 us (10%)
  starting transfers between devices  6.95 us (6%)
  local copies, waits for them, and re-layouts  3.97 us (4%)
  other arithmetic  1.28 us (1%)
    all_to_all x1, blocking collectives, local(): lax.all_to_all(packed, ('dp', 'expert'), split_axis=0, concat_axis=0, til...  32.9 us
    all_to_all x1, waiting for transfers between devices, local(): lax.all_to_all(result, ('dp', 'expert'), split_axis=0, concat_axis=0, til...  24.9 us
    reduce_scatter x1, waiting for transfers between devices, local(): lax.psum_scatter(partial_value, 'tensor', scatter_dimension=1, tiled=True)  10.6 us
    all_gather x1, waiting for transfers between devices, local(): owner_rows = jnp.concatenate(lax.all_gather(owner_rows, 'tensor'), axis=1)  7.52 us
    all_to_all x1, starting transfers between devices, local(): lax.all_to_all(result, ('dp', 'expert'), split_axis=0, concat_axis=0, til...  6.9 us
    dot_general x1, matrix products, local(): jnp.dot(hidden, w_down, preferred_element_type=jnp.float32)  6.6 us
    dot_general x1, matrix products, local(): gated = jnp.dot(owner_rows, w_gate, preferred_element_type=jnp.float32)  3.16 us
    all_gather x1, local copies, waits for them, and re-layouts, local(): owner_rows = jnp.concatenate(lax.all_gather(owner_rows, 'tensor'), axis=1)  2.8 us
  transfers between devices with their start and end apart: 3, of which 3 were waited for; matrix products, arithmetic and copies ran while one was open for 0% of the time, Pallas kernels for 0%

profile of v1, /device:TPU:0, one launch (start us, length us, event | category | flops | bytes accessed | tf_op | source)
XLA Modules:
  0.0 112.9 jit_solution(3459338048239512679)
XLA Ops:
  6.5 0.0 copy-start
  6.5 0.0 all-gather.2.cloned.1.call-start
  6.5 0.8 copy.30
  7.3 0.1 eq.51
  7.4 0.1 fusion.25
  7.5 0.2 reduce_window_sum.11
  7.7 0.2 select_reduce_fusion
  7.8 0.1 reduce_sum.42
  7.9 0.1 copy.31
  8.0 0.7 bitcast_add_fusion
  8.7 0.1 copy.32
  8.8 0.1 fusion.23
  8.9 0.0 copy-done
  8.9 0.4 convolution_convert_fusion.1
  9.3 32.9 %all_to_all.10 = bf16[16,16,1792]{2,1,0:T(8,128)(2,1)} all-to-all(bf16[16,16,1792]{2,1,0:T(8,128)(2,1)S(1)} %bitcast.42), channel_id=1, replica_groups=mesh['dp'=4,'expert'=4,'tensor'=2] {'dp','expert'}, dimensions={0} | all-to-all | bytes 1835008 | tf_op jit(solution)/shard_map/all_to_all | solution.py:30
  42.2 0.0 all-gather.2.cloned.1.call-update
  42.2 0.0 reduce-scatter.2.cloned.1.call-start
  42.3 7.5 %all-gather.2.cloned.1.call-done = bf16[2,256,1792]{2,1,0:T(8,128)(2,1)} async-done(((bf16[1,256,1792]{2,1,0:T(8,128)(2,1)}), bf16[2,256,1792]{2,1,0:T(8,128)(2,1)}) %all-gather.2.cloned.1.call-update) | async-done | bytes 1835024 | tf_op jit(solution)/shard_map/all_gather | solution.py:32
  49.8 2.8 %copy.34 = bf16[2,256,1792]{1,2,0:T(8,128)(2,1)S(1)} copy(bf16[2,256,1792]{2,1,0:T(8,128)(2,1)} %all-gather.2.cloned.1.call-done) | data formatting | bytes 3670016 | tf_op jit(solution)/shard_map/all_gather | solution.py:32
  52.6 3.2 %fusion.3 = f32[256,512]{1,0:T(8,128)S(1)} fusion(bf16[256,3584]{0,1:T(8,128)(2,1)S(1)} %bitcast.43, bf16[1,3584,512]{2,1,0:T(8,128)(2,1)} %param.7), kind=kOutput, calls=%fused_computation.4 | convolution fusion | flops 939524096 | bytes 6029312 | tf_op jit(solution)/shard_map/dot_general | solution.py:33
  55.8 6.6 %convolution_convert_fusion = bf16[256,3584]{1,0:T(8,128)(2,1)} fusion(bf16[1,512,3584]{2,1,0:T(8,128)(2,1)} %param.9, bf16[256,3584]{0,1:T(8,128)(2,1)S(1)} %bitcast.44, bf16[1,3584,512]{2,1,0:T(8,128)(2,1)} %param.8, f32[256,512]{1,0:T(8,128)S(1)} %fusion.3), kind=kOutput, calls=%fused_computation | convolution fusion | flops 1880752128 | bytes 11534336 | tf_op jit(solution)/shard_map/dot_general | solution.py:36
  62.4 0.0 copy-start.1
  62.4 0.0 reduce-scatter.2.cloned.1.call-update
  62.4 10.6 %reduce-scatter.2.cloned.1.call-done = bf16[256,1792]{1,0:T(8,128)(2,1)} async-done(((bf16[256,3584]{1,0:T(8,128)(2,1)}), bf16[256,1792]{1,0:T(8,128)(2,1)}) %reduce-scatter.2.cloned.1.call-update) | async-done | bytes 917520 | tf_op jit(solution)/shard_map/reduce_scatter | solution.py:38
  73.0 6.9 %all-to-all-start.1 = ((bf16[16,16,1792]{2,1,0:T(8,128)(2,1)}), bf16[16,16,1792]{2,1,0:T(8,128)(2,1)S(1)}, u32[]{:S(2)}, u32[]{:S(2)}) async-start(bf16[16,16,1792]{2,1,0:T(8,128)(2,1)} %bitcast.45), calls=%async_computation.2 | async-start | bytes 1835008 | tf_op jit(solution)/shard_map/all_to_all | solution.py:44
  80.0 0.0 copy-done.1
  80.0 0.1 copy.35
  80.1 24.9 %all-to-all-done.1 = bf16[16,16,1792]{2,1,0:T(8,128)(2,1)S(1)} async-done(((bf16[16,16,1792]{2,1,0:T(8,128)(2,1)}), bf16[16,16,1792]{2,1,0:T(8,128)(2,1)S(1)}, u32[]{:S(2)}, u32[]{:S(2)}) %all-to-all-start.1) | async-done | bytes 917536 | tf_op jit(solution)/shard_map/all_to_all | solution.py:44
  104.9 1.1 fusion.8
  (2 shorter events, 0.0 us)
Async XLA Ops:
  6.5 2.4 %copy-start = (bf16[1,16,1792]{2,1,0:T(8,128)(2,1)S(1)}, bf16[1,16,1792]{2,1,0:T(8,128)(2,1)}, u32[]{:S(2)}) copy-start(bf16[1,16,1792]{2,1,0:T(8,128)(2,1)} %param.6) | copy-start | bytes 172036
  6.5 43.3 %all-gather.2.cloned.1.call-start = ((), (), s32[]{:S(2)}) async-start(), calls=%async_computation.3 | async-start | bytes 2752512 | tf_op jit(solution)/shard_map/all_gather | solution.py:32
  42.2 30.8 %reduce-scatter.2.cloned.1.call-start = ((), (), s32[]{:S(2)}) async-start(), calls=%async_computation.4 | async-start | bytes 2752512 | tf_op jit(solution)/shard_map/reduce_scatter | solution.py:38
  62.4 17.6 %copy-start.1 = (s32[1,16,8]{1,2,0:T(8,128)S(1)}, s32[1,16,8]{1,2,0:T(8,128)}, u32[]{:S(2)}) copy-start(s32[1,16,8]{1,2,0:T(8,128)} %param.11) | copy-start | bytes 1540
  73.0 31.9 %all-to-all-start.1 = ((bf16[16,16,1792]{2,1,0:T(8,128)(2,1)}), bf16[16,16,1792]{2,1,0:T(8,128)(2,1)S(1)}, u32[]{:S(2)}, u32[]{:S(2)}) async-start(bf16[16,16,1792]{2,1,0:T(8,128)(2,1)} %bitcast.45), calls=%async_computation.2 | async-start | bytes 1835008 | tf_op jit(solution)/shard_map/all_to_all | solution.py:44
Sparse Core Ops, SparseCore 0:
  42.4 7.3 all-gather.1
  62.5 10.4 reduce-scatter.1
